TPU v7x, 32 devices: a 4x4x1 block of a 4x4x8 slice. The times are simulated.
32 devices in a mesh: rep: 2 (over z, core), dp: 16 (over x, y).
Axes of the slice: x: 4, y: 4, z: 1, core: 2. Of those that a mesh axis runs over, the one named last changes fastest.
The devices are a block of a 4x4x8 slice.
Arguments:
- x: bfloat16 [32, 2048, 768], P(('rep', 'dp')), parts along dimension 0
- dy: bfloat16 [32, 2048, 768], P(('rep', 'dp')), parts along dimension 0
- w_gate: bfloat16 [2, 768, 1792], replicated
- w_up: bfloat16 [2, 768, 1792], replicated
- w_down: bfloat16 [2, 1792, 768], replicated
- m_w_gate: float32 [2, 768, 1792], replicated
- m_w_up: float32 [2, 768, 1792], replicated
- m_w_down: float32 [2, 1792, 768], replicated
- v_w_gate: float32 [2, 768, 1792], replicated
- v_w_up: float32 [2, 768, 1792], replicated
- v_w_down: float32 [2, 1792, 768], replicated
Outputs:
- output 1: bfloat16 [4, 768, 1792], P('rep'), parts along dimension 0
- output 2: bfloat16 [4, 768, 1792], P('rep'), parts along dimension 0
- output 3: bfloat16 [4, 1792, 768], P('rep'), parts along dimension 0
- output 4: float32 [4, 768, 1792], P('rep'), parts along dimension 0
- output 5: float32 [4, 768, 1792], P('rep'), parts along dimension 0
- output 6: float32 [4, 1792, 768], P('rep'), parts along dimension 0
- output 7: float32 [4, 768, 1792], P('rep'), parts along dimension 0
- output 8: float32 [4, 768, 1792], P('rep'), parts along dimension 0
- output 9: float32 [4, 1792, 768], P('rep'), parts along dimension 0
There are 2 independent parts. A program takes and returns all parts, laid end to end along the dimension named above; an argument that names none is the same for every part.
All inputs are finite; a program needn't handle non-finite values.
Results may differ from a plain program's by a relative error of at most 0.022.
Values are sent between devices in bfloat16 or wider.
A program may use at most 768 MiB of HBM per device.

v0:
```python
import jax
import jax.numpy as jnp
from jax import lax
from jax.sharding import PartitionSpec as P

NAMES = ("w_gate", "w_up", "w_down")


def matmul(a, w):
    return jnp.dot(a, w, preferred_element_type=jnp.float32).astype(jnp.bfloat16)


def normed(h):
    wide = h.astype(jnp.float32)
    scale = lax.rsqrt(jnp.mean(wide**2, -1, keepdims=True) + 1e-6)
    return (wide * scale).astype(jnp.bfloat16)


def layer(h, w):
    a = normed(h)
    gate = jnp.dot(a, w["w_gate"], preferred_element_type=jnp.float32)
    up = jnp.dot(a, w["w_up"], preferred_element_type=jnp.float32)
    return h + matmul((jax.nn.silu(gate) * up).astype(jnp.bfloat16), w["w_down"])


def adamw(w, m, v, g):
    m = 0.9 * m + 0.1 * g
    v = 0.95 * v + 0.05 * g * g
    step = m * lax.rsqrt(v + 1e-8) + 0.1 * w
    return (w - 0.02 * step).astype(jnp.bfloat16), m, v


def clipped(gradients, sum_of_squares, count):
    factor = jnp.minimum(1.0, 0.5 * lax.rsqrt(sum_of_squares / count + 1e-30))
    return [g * factor for g in gradients]


def solution(mesh):
    def step(x, dy, *arrays):
        weights, m, v = (arrays[i : i + 3] for i in (0, 3, 6))
        layers = weights[0].shape[0]
        h, kept = x[0], []
        for number in range(layers):
            kept.append(h)
            h = layer(h, {name: w[number] for name, w in zip(NAMES, weights, strict=True)})
        by_h, summed = dy[0], [None] * layers
        for number in reversed(range(layers)):
            _, back = jax.vjp(lambda w, h: layer(h, w), {name: w[number] for name, w in zip(NAMES, weights, strict=True)}, kept[number])
            by_w, by_h = back(by_h)
            summed[number] = [lax.psum(by_w[name], "dp") for name in NAMES]
        gradients = [jnp.stack([summed[number][i] for number in range(layers)]).astype(jnp.float32) for i in range(3)]
        gradients = clipped(gradients, sum(jnp.sum(g * g) for g in gradients), sum(g.size for g in gradients))
        new = [adamw(w.astype(jnp.float32), m, v, g) for w, m, v, g in zip(weights, m, v, gradients, strict=True)]
        return tuple(one[which] for which in range(3) for one in new)

    return jax.shard_map(
        step,
        mesh=mesh,
        in_specs=(P(("rep", "dp"), None, None),) * 2 + (P(None, None, None),) * 9,
        out_specs=(P("rep", None, None),) * 9,
        check_vma=False,
    )
```

profile of v0, /device:TPU:97, one launch (start us, length us, event | category | flops | bytes accessed | tf_op | source)
XLA Modules:
  0.0 504.8 jit_solution(11393064382411857210)
XLA Ops:
  7.2 0.1 all-reduce.3.cloned.1.call-start
  7.3 3.2 copy.20
  10.5 0.0 copy-start
  10.5 0.7 fusion.36
  11.2 5.0 copy.21
  16.2 10.4 %convolution_convert_fusion.1 = bf16[2048,1792]{1,0:T(8,128)(2,1)} fusion(bf16[1,2048,768]{2,1,0:T(8,128)(2,1)} %param.12, bf16[2,1792,768]{2,1,0:T(8,128)(2,1)} %param.15), kind=kOutput, calls=%fused_computation.66 | convolution fusion | flops 5640814592 | bytes 13238272 | tf_op jit(solution)/shard_map/transpose(jvp())/dot_general | solution.py:10
  26.5 0.0 copy-done.5
  26.5 11.1 %fusion.77 = f32[2048,1792]{1,0:T(8,128)} fusion(bf16[2,768,1792]{2,1,0:T(8,128)(2,1)} %param.13, bf16[1,2048,768]{2,1,0:T(8,128)(2,1)S(1)} %copy-done.5, f32[2048]{0:T(1024)S(1)} %add_rsqrt_fusion), kind=kOutput, calls=%fused_computation.111 | convolution fusion | flops 5641863168 | bytes 20586496 | tf_op jit(solution)/shard_map/dot_general | solution.py:21
  37.6 0.0 copy-done.12
  37.6 0.0 slice-done
  37.6 0.0 slice-done.1
  37.6 16.2 %multiply_convert_fusion.1 = (bf16[2048,1792]{1,0:T(8,128)(2,1)}, f32[2048,1792]{1,0:T(8,128)}) fusion(f32[2048,1792]{1,0:T(8,128)} %fusion.77, bf16[2,768,1792]{2,1,0:T(8,128)(2,1)S(1)} %bitcast.77, bf16[1,2048,768]{2,1,0:T(8,128)(2,1)} %param.11, f32[2048]{0:T(1024)S(1)} %add_rsqrt_fusion), kind=kOutput, calls=%fused_computation.20 | convolution fusion | flops 5663883264 | bytes 42606592 | tf_op jit(solution)/shard_map/dot_general | solution.py:22
  53.9 0.0 copy-done
  53.9 9.7 %fusion.40 = (f32[2048]{0:T(1024)S(1)}, bf16[2048,768]{0,1:T(8,128)(2,1)S(1)}) fusion(bf16[2048,1792]{1,0:T(8,128)(2,1)} %get-tuple-element.24, bf16[2,1792,768]{2,1,0:T(8,128)(2,1)} %param.15, bf16[1,2048,768]{1,2,0:T(8,128)(2,1)S(1)} %copy.20), kind=kOutput, calls=%fused_computation.73 | convolution fusion | flops 5645006848 | bytes 16392192 | tf_op jit(solution)/shard_map/dot_general | solution.py:10
  63.5 0.0 copy-start.7
  63.6 0.0 copy-start.10
  63.6 1.6 copy-done.7
  65.2 0.0 copy-done.10
  65.2 9.3 %fusion.66 = f32[2048,1792]{1,0:T(8,128)} fusion(bf16[2,768,1792]{2,1,0:T(8,128)(2,1)S(1)} %bitcast.77, bf16[2048,768]{0,1:T(8,128)(2,1)S(1)} %get-tuple-element.27, f32[2048]{0:T(1024)S(1)} %fusion.100), kind=kOutput, calls=%fused_computation.100 | convolution fusion | flops 5641863168 | bytes 20586496 | tf_op jit(solution)/shard_map/jvp()/dot_general | solution.py:22
  74.5 23.3 %fusion.2 = (bf16[2048,1792]{1,0:T(8,128)(2,1)}, f32[2048,1792]{1,0:T(8,128)}) fusion(f32[2048,1792]{1,0:T(8,128)} %fusion.66, bf16[2048,1792]{1,0:T(8,128)(2,1)} %convolution_convert_fusion.1, bf16[2,768,1792]{2,1,0:T(8,128)(2,1)} %param.13, bf16[2048,768]{0,1:T(8,128)(2,1)} %copy-done.7, f32[2048]{0:T(1024)S(1)} %fusion.100), kind=kOutput, calls=%fused_computation.11 | convolution fusion | flops 5685903360 | bytes 49946624 | tf_op jit(solution)/shard_map/jvp()/dot_general | solution.py:21
  97.8 0.0 copy-done.8
  97.8 10.8 %fusion.57 = bf16[1,768,1792]{2,1,0:T(8,128)(2,1)} fusion(bf16[2048,1792]{1,0:T(8,128)(2,1)} %get-tuple-element.28, bf16[2048,768]{0,1:T(8,128)(2,1)S(1)} %copy-done.8, f32[2048]{0:T(1024)S(1)} %fusion.100), kind=kOutput, calls=%fused_computation.95 | convolution fusion | flops 5641863168 | bytes 13246464 | tf_op jit(solution)/shard_map/transpose(jvp())/dot_general | solution.py:21
  108.6 0.0 copy-done.14
  108.6 9.2 %convolution_convert_fusion.4 = bf16[2048,768]{0,1:T(8,128)(2,1)} fusion(bf16[2048,1792]{1,0:T(8,128)(2,1)S(1)} %copy-done.14, bf16[2,768,1792]{2,1,0:T(8,128)(2,1)} %param.13), kind=kOutput, calls=%fused_computation.82 | convolution fusion | flops 5637144576 | bytes 13238272 | tf_op jit(solution)/shard_map/transpose(jvp())/dot_general | solution.py:21
  117.8 14.1 %fusion.61 = bf16[1,1792,768]{2,1,0:T(8,128)(2,1)} fusion(bf16[1,2048,768]{2,1,0:T(8,128)(2,1)S(1)} %copy-done.6, f32[2048,1792]{1,0:T(8,128)} %fusion.66, f32[2048,1792]{1,0:T(8,128)} %get-tuple-element.29), kind=kOutput, calls=%fused_computation.99 | convolution fusion | flops 5660540928 | bytes 35258368 | tf_op jit(solution)/shard_map/transpose(jvp())/dot_general | solution.py:10
  131.9 12.5 %fusion.60 = bf16[1,768,1792]{2,1,0:T(8,128)(2,1)} fusion(bf16[2048,1792]{1,0:T(8,128)(2,1)} %convolution_convert_fusion.1, bf16[2048,768]{0,1:T(8,128)(2,1)S(1)} %copy-done.9, f32[2048]{0:T(1024)S(1)} %fusion.100, f32[2048,1792]{1,0:T(8,128)} %get-tuple-element.29), kind=kOutput, calls=%fused_computation.98 | convolution fusion | flops 5665259520 | bytes 27926528 | tf_op jit(solution)/shard_map/transpose(jvp())/dot_general | solution.py:22
  144.4 0.0 slice-done.2
  144.4 0.0 copy-start.2
  144.4 14.0 %fusion.42 = (f32[2048]{0:T(1024)S(1)}, bf16[2048,768]{0,1:T(8,128)(2,1)}) fusion(bf16[2048,768]{0,1:T(8,128)(2,1)} %copy-done.7, bf16[2048,768]{0,1:T(8,128)(2,1)} %convolution_convert_fusion.4, bf16[2,768,1792]{2,1,0:T(8,128)(2,1)S(1)} %bitcast.79, bf16[2048,1792]{1,0:T(8,128)(2,1)} %convolution_convert_fusion.1, f32[2048,1792]{1,0:T(8,128)} %get-tuple-element.29), kind=kOutput, calls=%fused_computation.75 | convolution fusion | flops 5668599808 | bytes 34217984 | tf_op jit(solution)/shard_map/transpose(jvp())/dot_general | solution.py:22
  158.5 0.0 slice-start.4
  158.5 5.2 %fusion.51 = bf16[2048,768]{0,1:T(8,128)(2,1)S(1)} fusion(bf16[2048,768]{0,1:T(8,128)(2,1)} %copy-done.7, bf16[2048,768]{0,1:T(8,128)(2,1)} %get-tuple-element.31, bf16[1,2048,768]{1,2,0:T(8,128)(2,1)S(1)} %copy-done.2, f32[2048]{0:T(1024)S(1)} %multiply_multiply_fusion.3, f32[2048]{0:T(1024)S(1)} %fusion.100), kind=kLoop, calls=%fused_computation.90 | loop fusion | flops 11010048 | bytes 12599296 | tf_op jit(solution)/shard_map/transpose(jvp())/add_any | solution.py:14
  163.6 0.0 slice-start.5
  163.6 9.4 %fusion.58 = bf16[1,1792,768]{2,1,0:T(8,128)(2,1)} fusion(bf16[2048,1792]{1,0:T(8,128)(2,1)} %get-tuple-element.24, bf16[2048,768]{0,1:T(8,128)(2,1)S(1)} %fusion.51), kind=kOutput, calls=%fused_computation.96 | convolution fusion | flops 5638520832 | bytes 13238272 | tf_op jit(solution)/shard_map/transpose(jvp())/dot_general | solution.py:10
  173.1 6.4 %convolution_convert_fusion = bf16[2048,1792]{1,0:T(8,128)(2,1)S(1)} fusion(bf16[2048,768]{0,1:T(8,128)(2,1)S(1)} %fusion.51, bf16[2,1792,768]{2,1,0:T(8,128)(2,1)S(1)} %bitcast.81), kind=kOutput, calls=%fused_computation.65 | convolution fusion | flops 5640814592 | bytes 13238272 | tf_op jit(solution)/shard_map/transpose(jvp())/dot_general | solution.py:10
  179.5 0.0 copy-done.1
  179.5 0.0 copy-done.13
  179.5 0.0 copy-start.15
  179.5 14.2 %fusion.59 = bf16[1,768,1792]{2,1,0:T(8,128)(2,1)} fusion(bf16[2048,1792]{1,0:T(8,128)(2,1)S(1)} %convolution_convert_fusion, bf16[1,2048,768]{1,2,0:T(8,128)(2,1)S(1)} %copy-done.1, f32[2048]{0:T(1024)S(1)} %copy-done.13, f32[2048,1792]{1,0:T(8,128)} %fusion.77), kind=kOutput, calls=%fused_computation.97 | convolution fusion | flops 5665259520 | bytes 27926528 | tf_op jit(solution)/shard_map/transpose(jvp())/dot_general | solution.py:22
  193.7 0.0 copy-done.15
  193.7 17.0 %fusion.54 = bf16[1,768,1792]{2,1,0:T(8,128)(2,1)} fusion(f32[2048,1792]{1,0:T(8,128)} %fusion.77, f32[2048,1792]{1,0:T(8,128)} %get-tuple-element.25, bf16[2048,1792]{1,0:T(8,128)(2,1)} %copy-done.15, bf16[1,2048,768]{1,2,0:T(8,128)(2,1)S(1)} %copy-done.1, f32[2048]{0:T(1024)S(1)} %copy-done.13), kind=kOutput, calls=%fused_computation.94 | convolution fusion | flops 5683609600 | bytes 42606592 | tf_op jit(solution)/shard_map/transpose(jvp())/dot_general | solution.py:21
  210.7 0.1 all-reduce.3.cloned.1.call-update
  210.8 209.8 %all-reduce.3.cloned.1.call-done = (bf16[1,768,1792]{2,1,0:T(8,128)(2,1)}, bf16[1,768,1792]{2,1,0:T(8,128)(2,1)}, bf16[1,768,1792]{2,1,0:T(8,128)(2,1)}, bf16[1,...) async-done(((bf16[1,768,1792]{2,1,0:T(8,128)(2,1)}, bf16[1,768,1792]{2,1,0:T(8,128)(2,1)}, bf16[1,768,1792]{2,1,0:T(8,128)(2,1)}, ...) | async-done | bytes 16515088 | tf_op jit(solution)/shard_map/psum | solution.py:50
  420.6 6.2 %fusion.22 = f32[]{:T(128)} fusion(bf16[1,1792,768]{2,1,0:T(8,128)(2,1)} %get-tuple-element.13, bf16[1,1792,768]{2,1,0:T(8,128)(2,1)} %get-tuple-element.14), kind=kLoop, calls=%fused_computation.46 | loop fusion | flops 11010047 | bytes 5505028 | tf_op jit(solution)/shard_map/reduce_sum | solution.py:52
  426.8 6.0 %fusion.21 = f32[]{:T(128)} fusion(bf16[1,768,1792]{2,1,0:T(8,128)(2,1)} %get-tuple-element.11, bf16[1,768,1792]{2,1,0:T(8,128)(2,1)} %get-tuple-element.12), kind=kLoop, calls=%fused_computation.45 | loop fusion | flops 11010047 | bytes 5505028 | tf_op jit(solution)/shard_map/reduce_sum | solution.py:52
  432.8 0.0 copy-done.4
  432.8 3.4 fusion.20
  438.2 21.9 %fusion.28 = (bf16[2,1792,768]{2,1,0:T(8,128)(2,1)}, f32[2,1792,768]{2,1,0:T(8,128)}, f32[2,1792,768]{2,1,0:T(8,128)}) fusion(bf16[2,1792,768]{2,1,0:T(8,128)(2,1)} %param.15, f32[]{:T(128)S(6)} %min_shard_map.3, bf16[1,1792,768]{2,1,0:T(8,128)(2,1)} %get-tuple-element.13, bf16[1,1792,768]{2,1,0:T(8,128)(2,1)} %get-tuple-element.14, ...), kind=kLoop, calls=%fused_computation.52 | loop fusion | flops 55050240 | bytes 60555268 | tf_op jit(solution)/shard_map/convert_element_type | solution.py:30
  460.2 37.3 %fusion.19 = (bf16[2,768,1792]{2,1,0:T(8,128)(2,1)}, f32[2,768,1792]{2,1,0:T(8,128)}, f32[2,768,1792]{2,1,0:T(8,128)}, bf16[2,768,1792]{2,1,0:T(8,128)(2,1)}, f3...) fusion(bf16[2,768,1792]{2,1,0:T(8,128)(2,1)} %param.13, f32[]{:T(128)S(6)} %min_shard_map.3, ...), kind=kLoop, calls=%fused_computation.43 | loop fusion | flops 110100480 | bytes 121110528 | tf_op jit(solution)/shard_map/convert_element_type | solution.py:30
  (29 shorter events, 0.1 us)
Async XLA Ops:
  7.2 413.4 %all-reduce.3.cloned.1.call-start = ((), (), s32[]{:S(2)}) async-start(), calls=%async_computation | async-start | bytes 33030144 | tf_op jit(solution)/shard_map/psum | solution.py:50
  10.5 43.4 %copy-start = (bf16[1,2048,768]{1,2,0:T(8,128)(2,1)}, bf16[1,2048,768]{1,2,0:T(8,128)(2,1)S(1)}, u32[]{:S(2)}) copy-start(bf16[1,2048,768]{1,2,0:T(8,128)(2,1)S(1)} %copy.20) | copy-start | bytes 9437188
  11.1 26.5 %copy-start.12 = (f32[2048]{0:T(1024)}, f32[2048]{0:T(1024)S(1)}, u32[]{:S(2)}) copy-start(f32[2048]{0:T(1024)S(1)} %add_rsqrt_fusion) | copy-start | bytes 24580
  16.2 10.4 %copy-start.5 = (bf16[1,2048,768]{2,1,0:T(8,128)(2,1)S(1)}, bf16[1,2048,768]{2,1,0:T(8,128)(2,1)}, u32[]{:S(2)}) copy-start(bf16[1,2048,768]{2,1,0:T(8,128)(2,1)} %param.11) | copy-start | bytes 9437188
  16.2 21.4 %slice-start = ((s8[5505024]{0:T(1024)(128)(4,1)}), s8[4194304]{0:T(1024)(128)(4,1)S(1)}, s32[]{:S(2)}) async-start(s8[5505024]{0:T(1024)(128)(4,1)} %bitcast.76), calls=%async_computation.1 | async-start | bytes 8388608
  26.5 11.1 %slice-start.1 = ((s8[5505024]{0:T(1024)(128)(4,1)}), s8[1310720]{0:T(1024)(128)(4,1)S(1)}, s32[]{:S(2)}) async-start(s8[5505024]{0:T(1024)(128)(4,1)} %bitcast.76), calls=%async_computation.2 | async-start | bytes 2621440
  63.5 1.7 copy-start.7
  63.6 1.7 copy-start.10
  74.5 23.3 %copy-start.8 = (bf16[2048,768]{0,1:T(8,128)(2,1)S(1)}, bf16[2048,768]{0,1:T(8,128)(2,1)}, u32[]{:S(2)}) copy-start(bf16[2048,768]{0,1:T(8,128)(2,1)} %copy-done.7) | copy-start | bytes 9437188
  97.8 10.8 %copy-start.14 = (bf16[2048,1792]{1,0:T(8,128)(2,1)S(1)}, bf16[2048,1792]{1,0:T(8,128)(2,1)}, u32[]{:S(2)}) copy-start(bf16[2048,1792]{1,0:T(8,128)(2,1)} %get-tuple-element.28) | copy-start | bytes 22020100
  108.6 9.2 %copy-start.6 = (bf16[1,2048,768]{2,1,0:T(8,128)(2,1)S(1)}, bf16[1,2048,768]{2,1,0:T(8,128)(2,1)}, u32[]{:S(2)}) copy-start(bf16[1,2048,768]{2,1,0:T(8,128)(2,1)} %param.12) | copy-start | bytes 9437188
  117.8 14.1 %copy-start.9 = (bf16[2048,768]{0,1:T(8,128)(2,1)S(1)}, bf16[2048,768]{0,1:T(8,128)(2,1)}, u32[]{:S(2)}) copy-start(bf16[2048,768]{0,1:T(8,128)(2,1)} %copy-done.7) | copy-start | bytes 9437188
  117.8 26.6 %slice-start.2 = ((s8[5505024]{0:T(1024)(128)(4,1)}), s8[4194304]{0:T(1024)(128)(4,1)S(1)}, s32[]{:S(2)}) async-start(s8[5505024]{0:T(1024)(128)(4,1)} %bitcast.78), calls=%async_computation.3 | async-start | bytes 8388608
  131.9 12.5 %slice-start.3 = ((s8[5505024]{0:T(1024)(128)(4,1)}), s8[1310720]{0:T(1024)(128)(4,1)S(1)}, s32[]{:S(2)}) async-start(s8[5505024]{0:T(1024)(128)(4,1)} %bitcast.78), calls=%async_computation.4 | async-start | bytes 2621440
  144.4 14.0 %copy-start.11 = (f32[2048]{0:T(1024)S(1)}, f32[2048]{0:T(1024)}, u32[]{:S(2)}) copy-start(f32[2048]{0:T(1024)} %copy-done.10) | copy-start | bytes 24580
  144.4 14.0 %copy-start.2 = (bf16[1,2048,768]{1,2,0:T(8,128)(2,1)S(1)}, bf16[1,2048,768]{1,2,0:T(8,128)(2,1)}, u32[]{:S(2)}) copy-start(bf16[1,2048,768]{1,2,0:T(8,128)(2,1)} %copy.21) | copy-start | bytes 9437188
  158.5 14.6 %slice-start.4 = ((s8[5505024]{0:T(1024)(128)(4,1)}), s8[1310720]{0:T(1024)(128)(4,1)S(1)}, s32[]{:S(2)}) async-start(s8[5505024]{0:T(1024)(128)(4,1)} %bitcast.80), calls=%async_computation.5 | async-start | bytes 2621440
  163.6 9.4 %slice-start.5 = ((s8[5505024]{0:T(1024)(128)(4,1)}), s8[4194304]{0:T(1024)(128)(4,1)S(1)}, s32[]{:S(2)}) async-start(s8[5505024]{0:T(1024)(128)(4,1)} %bitcast.80), calls=%async_computation.6 | async-start | bytes 8388608
  173.1 6.4 %copy-start.1 = (bf16[1,2048,768]{1,2,0:T(8,128)(2,1)S(1)}, bf16[1,2048,768]{1,2,0:T(8,128)(2,1)}, u32[]{:S(2)}) copy-start(bf16[1,2048,768]{1,2,0:T(8,128)(2,1)} %copy-done) | copy-start | bytes 9437188
  173.1 6.4 %copy-start.13 = (f32[2048]{0:T(1024)S(1)}, f32[2048]{0:T(1024)}, u32[]{:S(2)}) copy-start(f32[2048]{0:T(1024)} %copy-done.12) | copy-start | bytes 24580
  179.5 14.2 %copy-start.15 = (bf16[2048,1792]{1,0:T(8,128)(2,1)}, bf16[2048,1792]{1,0:T(8,128)(2,1)S(1)}, u32[]{:S(2)}) copy-start(bf16[2048,1792]{1,0:T(8,128)(2,1)S(1)} %convolution_convert_fusion) | copy-start | bytes 22020100
  420.6 12.2 %copy-start.3 = (bf16[1,768,1792]{2,1,0:T(8,128)(2,1)S(1)}, bf16[1,768,1792]{2,1,0:T(8,128)(2,1)}, u32[]{:S(2)}) copy-start(bf16[1,768,1792]{2,1,0:T(8,128)(2,1)} %get-tuple-element.9) | copy-start | bytes 8257540
  420.6 12.2 %copy-start.4 = (bf16[1,768,1792]{2,1,0:T(8,128)(2,1)S(1)}, bf16[1,768,1792]{2,1,0:T(8,128)(2,1)}, u32[]{:S(2)}) copy-start(bf16[1,768,1792]{2,1,0:T(8,128)(2,1)} %get-tuple-element.10) | copy-start | bytes 8257540
Sparse Core Ops, SparseCore 0:
  210.9 209.6 all-reduce.2
where the time goes:
time: 512 us; the launch traced here: 505 us
  waiting for transfers between devices  210 us (41%)
  matrix products  187 us (37%)
  other arithmetic  80.7 us (16%)
  between operations  16.8 us (3%)
  local copies, waits for them, and re-layouts  9.95 us (2%)
    psum x1, waiting for transfers between devices, step(): summed[number] = [lax.psum(by_w[name], 'dp') for name in NAMES]  210 us
    dot_general x5, matrix products, layer(): gate = jnp.dot(a, w['w_gate'], preferred_element_type=jnp.float32)  71.4 us
    dot_general x5, matrix products, layer(): up = jnp.dot(a, w['w_up'], preferred_element_type=jnp.float32)  66.1 us
    convert_element_type x2, other arithmetic, adamw(): return ((w - 0.02 * step).astype(jnp.bfloat16), m, v)  59.2 us
    dot_general x5, matrix products, matmul(): jnp.dot(a, w, preferred_element_type=jnp.float32).astype(jnp.bfloat16)  50 us
    reduce_sum x3, other arithmetic, step(): jnp.sum(g * g)  15.7 us
  transfers between devices with their start and end apart: 1, of which 1 were waited for; matrix products, arithmetic and copies ran while one was open for 0% of the time, Pallas kernels for 0%

commit v1 on v0

v1 whole, which is shorter than its diff:
```python
import functools
import math

import jax
import jax.numpy as jnp
from jax import lax
from jax.experimental import pallas as pl
from jax.experimental.pallas import tpu as pltpu
from jax.sharding import PartitionSpec as P

NAMES = ("w_gate", "w_up", "w_down")
MESH = pl.DeviceIdType.MESH


def matmul(a, w):
    return jnp.dot(a, w, preferred_element_type=jnp.float32).astype(jnp.bfloat16)


def normed(h):
    wide = h.astype(jnp.float32)
    scale = lax.rsqrt(jnp.mean(wide**2, -1, keepdims=True) + 1e-6)
    return (wide * scale).astype(jnp.bfloat16)


def layer(h, w):
    a = normed(h)
    gate = jnp.dot(a, w["w_gate"], preferred_element_type=jnp.float32)
    up = jnp.dot(a, w["w_up"], preferred_element_type=jnp.float32)
    return h + matmul((jax.nn.silu(gate) * up).astype(jnp.bfloat16), w["w_down"])


def factor_kernel(n, count, *refs):
    shards, (out_ref, mine, slots, send_sems, recv_sems) = refs[:-5], refs[-5:]
    me = lax.axis_index("dp")
    barrier = pltpu.get_barrier_semaphore()
    for d in range(1, n):
        pl.semaphore_signal(barrier, inc=1, device_id={"dp": lax.rem(me + d, n)}, device_id_type=MESH)
    total = jnp.zeros((1, 128), jnp.float32)
    for ref in shards:
        g = ref[...].astype(jnp.float32)
        part = jnp.sum(g * g, axis=0, keepdims=True)
        for c in range(0, part.shape[1], 128):
            total = total + part[:, c : c + 128]
    mine[...] = jnp.broadcast_to(total, mine.shape)
    slots[me] = jnp.broadcast_to(total, mine.shape)
    pl.semaphore_wait(barrier, n - 1)
    copies = []
    for d in range(1, n):
        to = lax.rem(me + d, n)
        copy = pltpu.make_async_remote_copy(
            src_ref=mine, dst_ref=slots.at[me], send_sem=send_sems.at[d], recv_sem=recv_sems.at[d], device_id={"dp": to}, device_id_type=MESH
        )
        copy.start()
        copies.append(copy)
    for copy in copies:
        copy.wait_recv()
    for copy in copies:
        copy.wait_send()
    squares = jnp.zeros((8, 128), jnp.float32)
    for i in range(n):
        squares = squares + slots[i]
    squares = jnp.sum(squares[0:1], axis=1, keepdims=True)
    out_ref[...] = jnp.broadcast_to(jnp.minimum(1.0, 0.5 * lax.rsqrt(squares / count + 1e-30)), out_ref.shape)


def clip_factor(shards, n, count):
    return pl.pallas_call(
        functools.partial(factor_kernel, n, count),
        out_shape=jax.ShapeDtypeStruct((8, 128), jnp.float32),
        in_specs=[pl.BlockSpec(memory_space=pltpu.VMEM)] * len(shards),
        out_specs=pl.BlockSpec(memory_space=pltpu.VMEM),
        scratch_shapes=[
            pltpu.VMEM((8, 128), jnp.float32),
            pltpu.VMEM((n, 8, 128), jnp.float32),
            pltpu.SemaphoreType.DMA((n,)),
            pltpu.SemaphoreType.DMA((n,)),
        ],
        compiler_params=pltpu.CompilerParams(collective_id=0, has_side_effects=True, vmem_limit_bytes=16 * 2**20),
        cost_estimate=pl.CostEstimate(flops=10**7, bytes_accessed=2**20, transcendentals=0),
        name="clip_factor",
    )(*shards)


def adamw_kernel(f_ref, g_ref, w_ref, m_ref, v_ref, *rest):
    nw_ref, nm_ref, nv_ref = rest[-3:]
    f = f_ref[0:1, 0:1]
    g = g_ref[...].astype(jnp.float32) * f
    m = 0.9 * m_ref[0] + 0.1 * g
    v = 0.95 * v_ref[0] + 0.05 * g * g
    w = w_ref[0].astype(jnp.float32)
    nm_ref[0] = m
    nv_ref[0] = v
    nw_ref[0] = (w - 0.02 * (m * lax.rsqrt(v + 1e-8) + 0.1 * w)).astype(jnp.bfloat16)


def adamw(number, f, g, w, m, v, before):
    _, rows, cols = w.shape
    block = next(b for b in (128, 112, 96, 64, 32, 16) if rows % b == 0)
    whole = pl.BlockSpec((1, block, cols), lambda i: (number, i, 0))
    outs = [jax.ShapeDtypeStruct(a.shape, a.dtype) for a in (w, m, v)]
    size = rows * cols
    return pl.pallas_call(
        adamw_kernel,
        grid=(rows // block,),
        out_shape=outs,
        in_specs=[pl.BlockSpec((8, 128), lambda i: (0, 0)), pl.BlockSpec((block, cols), lambda i: (i, 0)), whole, whole, whole]
        + [pl.BlockSpec(memory_space=pl.ANY)] * len(before),
        out_specs=[whole] * 3,
        input_output_aliases={5 + i: i for i in range(len(before))},
        compiler_params=pltpu.CompilerParams(vmem_limit_bytes=32 * 2**20),
        cost_estimate=pl.CostEstimate(flops=16 * size * 40, bytes_accessed=22 * size, transcendentals=size),
        name="adamw",
    )(f, g, w, m, v, *before)


def solution(mesh):
    n = mesh.shape["dp"]

    def step(x, dy, *arrays):
        weights, m, v = (arrays[i : i + 3] for i in (0, 3, 6))
        layers = weights[0].shape[0]
        h, kept = x[0], []
        for number in range(layers):
            kept.append(h)
            h = layer(h, {name: w[number] for name, w in zip(NAMES, weights, strict=True)})
        by_h, shards = dy[0], {}
        for number in reversed(range(layers)):
            _, back = jax.vjp(lambda w, h: layer(h, w), {name: w[number] for name, w in zip(NAMES, weights, strict=True)}, kept[number])
            by_w, by_h = back(by_h)
            for i, name in reversed(list(enumerate(NAMES))):
                shards[number, i] = lax.psum_scatter(by_w[name], "dp", scatter_dimension=0, tiled=True)
        f = clip_factor(list(shards.values()), n, float(sum(w.size for w in weights)))
        new = [()] * 3
        for (number, i), shard in shards.items():
            g = lax.all_gather(shard, "dp", axis=0, tiled=True)
            new[i] = adamw(number, f, g, weights[i], m[i], v[i], new[i])
        return tuple(one[which] for which in range(3) for one in new)

    return jax.shard_map(
        step,
        mesh=mesh,
        in_specs=(P(("rep", "dp"), None, None),) * 2 + (P(None, None, None),) * 9,
        out_specs=(P("rep", None, None),) * 9,
        check_vma=False,
    )
```

time: 512 us -> 841 us (1.64)
  waiting for transfers between devices: 210 us -> 477 us
  other arithmetic: 80.7 us -> 6.67 us
  Pallas kernels: 0 us -> 68.9 us
  local copies, waits for them, and re-layouts: 9.95 us -> 70.8 us
    reduce_scatter x0 -> x6, waiting for transfers between devices: none -> 327 us  [step(): lax.psum_scatter(by_w[name], 'dp', scatter_dimension=0, tiled=True)]
    psum x1 -> x0, waiting for transfers between devices: 210 us -> none  [step(): summed[number] = [lax.psum(by_w[name], 'dp') for name in NAMES]]
    all_gather x0 -> x6, waiting for transfers between devices: none -> 149 us  [step(): g = lax.all_gather(shard, 'dp', axis=0, tiled=True)]
    pallas_call x0 -> x7, Pallas kernels: none -> 68.9 us  [the longest x6 61.9 us: adamw(): pl.pallas_call(adamw_kernel, grid=(rows // block,), out_shape=outs, in_sp...]
    unnamed x46 -> x86, local copies, waits for them, and re-layouts: 9.95 us -> 70.8 us
    convert_element_type x2 -> x0, other arithmetic: 59.2 us -> none  [adamw(): return ((w - 0.02 * step).astype(jnp.bfloat16), m, v)]
    reduce_sum x3 -> x0, other arithmetic: 15.7 us -> none  [step(): jnp.sum(g * g)]
  transfers between devices with their start and end apart: 1 -> 12, of which waited for: 1 -> 11; matrix products, arithmetic and copies ran while one was open for 0% -> 13% of each run, Pallas kernels for 0% -> 7%
where the time goes in v1:
time: 841 us; the launch traced here: 830 us
  waiting for transfers between devices  477 us (57%)
  matrix products  191 us (23%)
  local copies, waits for them, and re-layouts  70.8 us (8%)
  Pallas kernels  68.9 us (8%)
  between operations  14.9 us (2%)
    reduce_scatter x6, waiting for transfers between devices, step(): lax.psum_scatter(by_w[name], 'dp', scatter_dimension=0, tiled=True)  327 us
    all_gather x6, waiting for transfers between devices, step(): g = lax.all_gather(shard, 'dp', axis=0, tiled=True)  149 us
    unnamed x86, local copies, waits for them, and re-layouts  70.8 us
    dot_general x5, matrix products, layer(): gate = jnp.dot(a, w['w_gate'], preferred_element_type=jnp.float32)  69.9 us
    dot_general x5, matrix products, layer(): up = jnp.dot(a, w['w_up'], preferred_element_type=jnp.float32)  68.1 us
    pallas_call x6, Pallas kernels, adamw(): pl.pallas_call(adamw_kernel, grid=(rows // block,), out_shape=outs, in_sp...  61.9 us
    dot_general x5, matrix products, matmul(): jnp.dot(a, w, preferred_element_type=jnp.float32).astype(jnp.bfloat16)  52.7 us
  transfers between devices with their start and end apart: 12, of which 11 were waited for; matrix products, arithmetic and copies ran while one was open for 13% of the time, Pallas kernels for 7%

profile of v1, /device:TPU:97, one launch (start us, length us, event | category | flops | bytes accessed | tf_op | source)
XLA Modules:
  0.0 830.3 jit_solution(17940328343633279412)
XLA Ops:
  7.3 3.2 copy.29
  11.2 11.6 %convolution_convert_fusion.1 = bf16[2048,1792]{1,0:T(8,128)(2,1)} fusion(bf16[1,2048,768]{2,1,0:T(8,128)(2,1)} %param.12, bf16[2,1792,768]{2,1,0:T(8,128)(2,1)} %w_ref.11), kind=kOutput, calls=%fused_computation.30 | convolution fusion | flops 5640814592 | bytes 13238272 | tf_op jit(solution)/shard_map/transpose(jvp())/dot_general | solution.py:16
  22.8 9.2 %fusion.46 = f32[2048,1792]{1,0:T(8,128)} fusion(bf16[2,768,1792]{2,1,0:T(8,128)(2,1)S(1)} %bitcast.67, bf16[1,2048,768]{2,1,0:T(8,128)(2,1)S(1)} %copy-done.26, f32[2048]{0:T(1024)S(1)} %add_rsqrt_fusion), kind=kOutput, calls=%fused_computation.66 | convolution fusion | flops 5641863168 | bytes 20586496 | tf_op jit(solution)/shard_map/dot_general | solution.py:27
  32.0 15.3 %multiply_convert_fusion.1 = (bf16[2048,1792]{1,0:T(8,128)(2,1)}, f32[2048,1792]{1,0:T(8,128)}) fusion(f32[2048,1792]{1,0:T(8,128)} %fusion.46, bf16[2,768,1792]{2,1,0:T(8,128)(2,1)} %w_ref.9, bf16[1,2048,768]{2,1,0:T(8,128)(2,1)} %param.11, f32[2048]{0:T(1024)S(1)} %add_rsqrt_fusion), kind=kOutput, calls=%fused_computation.17 | convolution fusion | flops 5663883264 | bytes 42606592 | tf_op jit(solution)/shard_map/dot_general | solution.py:28
  47.4 8.7 %fusion.19 = (f32[2048]{0:T(1024)S(1)}, bf16[2048,768]{0,1:T(8,128)(2,1)S(1)}) fusion(bf16[2048,1792]{1,0:T(8,128)(2,1)} %get-tuple-element.45, bf16[2,1792,768]{2,1,0:T(8,128)(2,1)S(1)} %bitcast.63, bf16[1,2048,768]{1,2,0:T(8,128)(2,1)S(1)} %copy.29), kind=kOutput, calls=%fused_computation.37 | convolution fusion | flops 5645006848 | bytes 16392192 | tf_op jit(solution)/shard_map/dot_general | solution.py:16
  57.8 11.1 %fusion.37 = f32[2048,1792]{1,0:T(8,128)} fusion(bf16[2,768,1792]{2,1,0:T(8,128)(2,1)} %w_ref.9, bf16[2048,768]{0,1:T(8,128)(2,1)S(1)} %get-tuple-element.48, f32[2048]{0:T(1024)S(1)} %fusion.69), kind=kOutput, calls=%fused_computation.57 | convolution fusion | flops 5641863168 | bytes 20586496 | tf_op jit(solution)/shard_map/jvp()/dot_general | solution.py:28
  68.9 23.3 %fusion.2 = (bf16[2048,1792]{1,0:T(8,128)(2,1)}, f32[2048,1792]{1,0:T(8,128)}) fusion(f32[2048,1792]{1,0:T(8,128)} %fusion.37, bf16[2048,1792]{1,0:T(8,128)(2,1)} %convolution_convert_fusion.1, bf16[2,768,1792]{2,1,0:T(8,128)(2,1)} %w_ref.7, bf16[2048,768]{0,1:T(8,128)(2,1)} %copy-done.28, f32[2048]{0:T(1024)S(1)} %fusion.69), kind=kOutput, calls=%fused_computation.8 | convolution fusion | flops 5685903360 | bytes 49946624 | tf_op jit(solution)/shard_map/jvp()/dot_general | solution.py:27
  92.2 14.4 %fusion.22 = bf16[1792,768]{1,0:T(8,128)(2,1)} fusion(f32[2048,1792]{1,0:T(8,128)} %fusion.37, bf16[1,2048,768]{2,1,0:T(8,128)(2,1)S(1)} %copy-done.27, f32[2048,1792]{1,0:T(8,128)} %get-tuple-element.50), kind=kOutput, calls=%fused_computation.45 | convolution fusion | flops 5660540928 | bytes 35258368 | tf_op jit(solution)/shard_map/transpose(jvp())/dot_general | solution.py:16
  106.8 16.4 %fusion.23 = bf16[768,1792]{1,0:T(8,128)(2,1)} fusion(bf16[2048,1792]{1,0:T(8,128)(2,1)} %convolution_convert_fusion.1, bf16[2048,768]{0,1:T(8,128)(2,1)} %copy-done.28, f32[2048]{0:T(1024)S(1)} %fusion.69, f32[2048,1792]{1,0:T(8,128)} %get-tuple-element.50), kind=kOutput, calls=%fused_computation.46 | convolution fusion | flops 5665259520 | bytes 27926528 | tf_op jit(solution)/shard_map/transpose(jvp())/dot_general | solution.py:28
  123.3 10.2 %convolution_convert_fusion.4 = bf16[768,1792]{1,0:T(8,128)(2,1)} fusion(bf16[2048,1792]{1,0:T(8,128)(2,1)} %get-tuple-element.49, bf16[2048,768]{0,1:T(8,128)(2,1)S(1)} %copy-done.29, f32[2048]{0:T(1024)S(1)} %fusion.69), kind=kOutput, calls=%fused_computation.43 | convolution fusion | flops 5641863168 | bytes 13246464 | tf_op jit(solution)/shard_map/transpose(jvp())/dot_general | solution.py:27
  133.7 4.9 copy.30
  138.6 10.3 %convolution_convert_fusion.3 = bf16[2048,768]{0,1:T(8,128)(2,1)} fusion(bf16[2048,1792]{1,0:T(8,128)(2,1)} %get-tuple-element.49, bf16[2,768,1792]{2,1,0:T(8,128)(2,1)} %w_ref.7), kind=kOutput, calls=%fused_computation.42 | convolution fusion | flops 5637144576 | bytes 13238272 | tf_op jit(solution)/shard_map/transpose(jvp())/dot_general | solution.py:27
  148.9 13.8 %fusion.21 = (f32[2048]{0:T(1024)S(1)}, bf16[2048,768]{0,1:T(8,128)(2,1)}) fusion(bf16[2048,768]{0,1:T(8,128)(2,1)} %copy-done.28, bf16[2048,768]{0,1:T(8,128)(2,1)} %convolution_convert_fusion.3, bf16[2,768,1792]{2,1,0:T(8,128)(2,1)S(1)} %bitcast.65, bf16[2048,1792]{1,0:T(8,128)(2,1)} %convolution_convert_fusion.1, f32[2048,1792]{1,0:T(8,128)} %get-tuple-element.50), kind=kOutput, calls=%fused_computation.39 | convolution fusion | flops 5668599808 | bytes 34217984 | tf_op jit(solution)/shard_map/transpose(jvp())/dot_general | solution.py:28
  162.7 6.0 fusion.30
  170.4 9.3 %convolution_convert_fusion.2 = bf16[1792,768]{1,0:T(8,128)(2,1)} fusion(bf16[2048,1792]{1,0:T(8,128)(2,1)} %get-tuple-element.45, bf16[2048,768]{0,1:T(8,128)(2,1)S(1)} %fusion.30), kind=kOutput, calls=%fused_computation.41 | convolution fusion | flops 5638520832 | bytes 13238272 | tf_op jit(solution)/shard_map/transpose(jvp())/dot_general | solution.py:16
  179.8 8.8 %convolution_convert_fusion = bf16[2048,1792]{1,0:T(8,128)(2,1)S(1)} fusion(bf16[2048,768]{0,1:T(8,128)(2,1)} %copy-done.30, bf16[2,1792,768]{2,1,0:T(8,128)(2,1)} %w_ref.11), kind=kOutput, calls=%fused_computation.29 | convolution fusion | flops 5640814592 | bytes 13238272 | tf_op jit(solution)/shard_map/transpose(jvp())/dot_general | solution.py:16
  188.6 3.0 copy-done.35
  191.6 11.5 %fusion.28 = bf16[768,1792]{1,0:T(8,128)(2,1)} fusion(bf16[2048,1792]{1,0:T(8,128)(2,1)S(1)} %convolution_convert_fusion, bf16[1,2048,768]{1,2,0:T(8,128)(2,1)S(1)} %copy-done.25, f32[2048]{0:T(1024)S(1)} %copy-done.34, f32[2048,1792]{1,0:T(8,128)} %fusion.46), kind=kOutput, calls=%fused_computation.49 | convolution fusion | flops 5665259520 | bytes 27926528 | tf_op jit(solution)/shard_map/transpose(jvp())/dot_general | solution.py:28
  203.2 16.8 %fusion.25 = bf16[768,1792]{1,0:T(8,128)(2,1)} fusion(f32[2048,1792]{1,0:T(8,128)} %fusion.46, f32[2048,1792]{1,0:T(8,128)} %get-tuple-element.46, bf16[2048,1792]{1,0:T(8,128)(2,1)} %copy-done.35, bf16[1,2048,768]{1,2,0:T(8,128)(2,1)S(1)} %copy-done.25, f32[2048]{0:T(1024)S(1)} %copy-done.34), kind=kOutput, calls=%fused_computation.48 | convolution fusion | flops 5683609600 | bytes 42606592 | tf_op jit(solution)/shard_map/transpose(jvp())/dot_general | solution.py:27
  221.0 33.0 %reduce-scatter.9.cloned.1.call-done.refs_1_ = bf16[48,1792]{1,0:T(8,128)(2,1)} async-done(((bf16[768,1792]{1,0:T(8,128)(2,1)}), bf16[48,1792]{1,0:T(8,128)(2,1)}) %reduce-scatter.9.cloned.1.call-update) | async-done | bytes 172048 | tf_op jit(solution)/shard_map/reduce_scatter | solution.py:131
  254.1 73.4 %reduce-scatter.11.cloned.1.call-done.refs_2_ = bf16[48,1792]{1,0:T(8,128)(2,1)} async-done(((bf16[768,1792]{1,0:T(8,128)(2,1)}), bf16[48,1792]{1,0:T(8,128)(2,1)}) %reduce-scatter.11.cloned.1.call-update) | async-done | bytes 172048 | tf_op jit(solution)/shard_map/reduce_scatter | solution.py:131
  327.6 73.8 %reduce-scatter.13.cloned.1.call-done.refs_3_ = bf16[112,768]{1,0:T(8,128)(2,1)} async-done(((bf16[1792,768]{1,0:T(8,128)(2,1)}), bf16[112,768]{1,0:T(8,128)(2,1)}) %reduce-scatter.13.cloned.1.call-update) | async-done | bytes 172048 | tf_op jit(solution)/shard_map/reduce_scatter | solution.py:131
  401.6 73.8 %reduce-scatter.15.cloned.1.call-done.refs_4_ = bf16[48,1792]{1,0:T(8,128)(2,1)} async-done(((bf16[768,1792]{1,0:T(8,128)(2,1)}), bf16[48,1792]{1,0:T(8,128)(2,1)}) %reduce-scatter.15.cloned.1.call-update) | async-done | bytes 172048 | tf_op jit(solution)/shard_map/reduce_scatter | solution.py:131
  475.7 73.4 %reduce-scatter.17.cloned.1.call-done.refs_5_ = bf16[48,1792]{1,0:T(8,128)(2,1)} async-done(((bf16[768,1792]{1,0:T(8,128)(2,1)}), bf16[48,1792]{1,0:T(8,128)(2,1)}) %reduce-scatter.17.cloned.1.call-update) | async-done | bytes 172048 | tf_op jit(solution)/shard_map/reduce_scatter | solution.py:131
  554.7 7.0 clip_factor.1.f_ref
  561.7 30.7 %all-gather.17.cloned.1.call-done.g_ref = bf16[1792,768]{1,0:T(8,128)(2,1)} async-done(((bf16[112,768]{1,0:T(8,128)(2,1)}), bf16[1792,768]{1,0:T(8,128)(2,1)}) %all-gather.17.cloned.1.call-update) | async-done | bytes 2752528 | tf_op jit(solution)/shard_map/all_gather | solution.py:135
  592.4 4.1 copy-done
  596.5 2.6 copy-done.6
  600.9 12.0 %adamw.10 = (bf16[2,1792,768]{2,1,0:T(8,128)(2,1)}, f32[2,1792,768]{2,1,0:T(8,128)}, f32[2,1792,768]{2,1,0:T(8,128)}) custom-call(f32[8,128]{1,0:T(8,128)S(1)} %clip_factor.1.f_ref, bf16[1792,768]{1,0:T(8,128)(2,1)S(1)} %copy-done.15, bf16[2,1792,768]{2,1,0:T(8,128)(2,1)S(1)} %copy-done.6, f32[2,1792,768]{2,1,0:T(8,128)S(1)} %copy-done, f32[2,1792,768]{2,1,0:T(8,128)} %v_ref.11), custom_call_target="tpu_custom_call" | custom-call | flops 880803840 | bytes 30277632 | tf_op jit(solution)/shard_map/adamw/pallas_call | solution.py:102
  612.9 22.1 %all-gather.13.cloned.1.call-done.g_ref = bf16[768,1792]{1,0:T(8,128)(2,1)} async-done(((bf16[48,1792]{1,0:T(8,128)(2,1)}), bf16[768,1792]{1,0:T(8,128)(2,1)}) %all-gather.13.cloned.1.call-update) | async-done | bytes 2752528 | tf_op jit(solution)/shard_map/all_gather | solution.py:135
  635.0 4.1 copy-done.2
  639.1 2.6 copy-done.8
  643.5 9.5 %adamw.8 = (bf16[2,768,1792]{2,1,0:T(8,128)(2,1)}, f32[2,768,1792]{2,1,0:T(8,128)}, f32[2,768,1792]{2,1,0:T(8,128)}) custom-call(f32[8,128]{1,0:T(8,128)S(1)} %clip_factor.1.f_ref, bf16[768,1792]{1,0:T(8,128)(2,1)S(1)} %copy-done.16, bf16[2,768,1792]{2,1,0:T(8,128)(2,1)S(1)} %copy-done.8, f32[2,768,1792]{2,1,0:T(8,128)S(1)} %copy-done.2, f32[2,768,1792]{2,1,0:T(8,128)} %v_ref.9), custom_call_target="tpu_custom_call" | custom-call | flops 880803840 | bytes 30277632 | tf_op jit(solution)/shard_map/adamw/pallas_call | solution.py:102
  653.0 24.6 %all-gather.9.cloned.1.call-done.g_ref = bf16[768,1792]{1,0:T(8,128)(2,1)} async-done(((bf16[48,1792]{1,0:T(8,128)(2,1)}), bf16[768,1792]{1,0:T(8,128)(2,1)}) %all-gather.9.cloned.1.call-update) | async-done | bytes 2752528 | tf_op jit(solution)/shard_map/all_gather | solution.py:135
  677.6 4.1 copy-done.4
  681.7 2.6 copy-done.10
  686.1 9.5 %adamw.6 = (bf16[2,768,1792]{2,1,0:T(8,128)(2,1)}, f32[2,768,1792]{2,1,0:T(8,128)}, f32[2,768,1792]{2,1,0:T(8,128)}) custom-call(f32[8,128]{1,0:T(8,128)S(1)} %clip_factor.1.f_ref, bf16[768,1792]{1,0:T(8,128)(2,1)S(1)} %copy-done.17, bf16[2,768,1792]{2,1,0:T(8,128)(2,1)S(1)} %copy-done.10, f32[2,768,1792]{2,1,0:T(8,128)S(1)} %copy-done.4, f32[2,768,1792]{2,1,0:T(8,128)} %v_ref.7), custom_call_target="tpu_custom_call" | custom-call | flops 880803840 | bytes 30277632 | tf_op jit(solution)/shard_map/adamw/pallas_call | solution.py:102
  695.6 24.5 %all-gather.15.cloned.1.call-done.g_ref = bf16[1792,768]{1,0:T(8,128)(2,1)} async-done(((bf16[112,768]{1,0:T(8,128)(2,1)}), bf16[1792,768]{1,0:T(8,128)(2,1)}) %all-gather.15.cloned.1.call-update) | async-done | bytes 2752528 | tf_op jit(solution)/shard_map/all_gather | solution.py:135
  720.0 4.1 copy-done.1
  724.2 2.6 copy-done.7
  728.5 12.0 %adamw.11 = (bf16[2,1792,768]{2,1,0:T(8,128)(2,1)}, f32[2,1792,768]{2,1,0:T(8,128)}, f32[2,1792,768]{2,1,0:T(8,128)}) custom-call(f32[8,128]{1,0:T(8,128)S(1)} %clip_factor.1.f_ref, bf16[1792,768]{1,0:T(8,128)(2,1)S(1)} %copy-done.12, bf16[2,1792,768]{2,1,0:T(8,128)(2,1)S(1)} %copy-done.7, ...), custom_call_target="tpu_custom_call", output_to_operand_aliasing={{0}: (5, {}), {1}: (6, {}), {2}: (7, {})} | custom-call | flops 880803840 | bytes 30277632 | tf_op jit(solution)/shard_map/adamw/pallas_call | solution.py:102
  740.5 22.2 %all-gather.11.cloned.1.call-done.g_ref = bf16[768,1792]{1,0:T(8,128)(2,1)} async-done(((bf16[48,1792]{1,0:T(8,128)(2,1)}), bf16[768,1792]{1,0:T(8,128)(2,1)}) %all-gather.11.cloned.1.call-update) | async-done | bytes 2752528 | tf_op jit(solution)/shard_map/all_gather | solution.py:135
  762.6 4.1 copy-done.3
  766.8 2.6 copy-done.9
  771.1 9.5 %adamw.9 = (bf16[2,768,1792]{2,1,0:T(8,128)(2,1)}, f32[2,768,1792]{2,1,0:T(8,128)}, f32[2,768,1792]{2,1,0:T(8,128)}) custom-call(f32[8,128]{1,0:T(8,128)S(1)} %clip_factor.1.f_ref, bf16[768,1792]{1,0:T(8,128)(2,1)S(1)} %copy-done.13, bf16[2,768,1792]{2,1,0:T(8,128)(2,1)S(1)} %copy-done.9, ...), custom_call_target="tpu_custom_call", output_to_operand_aliasing={{0}: (5, {}), {1}: (6, {}), {2}: (7, {})} | custom-call | flops 880803840 | bytes 30277632 | tf_op jit(solution)/shard_map/adamw/pallas_call | solution.py:102
  780.6 24.5 %all-gather.7.cloned.1.call-done.g_ref = bf16[768,1792]{1,0:T(8,128)(2,1)} async-done(((bf16[48,1792]{1,0:T(8,128)(2,1)}), bf16[768,1792]{1,0:T(8,128)(2,1)}) %all-gather.7.cloned.1.call-update) | async-done | bytes 2752528 | tf_op jit(solution)/shard_map/all_gather | solution.py:135
  805.1 4.1 copy-done.5
  813.5 9.5 %adamw.7 = (bf16[2,768,1792]{2,1,0:T(8,128)(2,1)}, f32[2,768,1792]{2,1,0:T(8,128)}, f32[2,768,1792]{2,1,0:T(8,128)}) custom-call(f32[8,128]{1,0:T(8,128)S(1)} %clip_factor.1.f_ref, bf16[768,1792]{1,0:T(8,128)(2,1)S(1)} %copy-done.14, bf16[2,768,1792]{2,1,0:T(8,128)(2,1)S(1)} %copy-done.11, ...), custom_call_target="tpu_custom_call", output_to_operand_aliasing={{0}: (5, {}), {1}: (6, {}), {2}: (7, {})} | custom-call | flops 880803840 | bytes 30277632 | tf_op jit(solution)/shard_map/adamw/pallas_call | solution.py:102
  (104 shorter events, 25.1 us)
Async XLA Ops:
  7.2 213.0 %reduce-scatter.7.cloned.1.call-start = ((), (), s32[]{:S(2)}) async-start(), calls=%async_computation.6 | async-start | bytes 2924544 | tf_op jit(solution)/shard_map/reduce_scatter | solution.py:131
  10.5 36.9 %copy-start.24 = (bf16[1,2048,768]{1,2,0:T(8,128)(2,1)}, bf16[1,2048,768]{1,2,0:T(8,128)(2,1)S(1)}, u32[]{:S(2)}) copy-start(bf16[1,2048,768]{1,2,0:T(8,128)(2,1)S(1)} %copy.29) | copy-start | bytes 9437188
  10.5 12.4 %slice-start.4 = ((s8[5505024]{0:T(1024)(128)(4,1)}), s8[4194304]{0:T(1024)(128)(4,1)S(1)}, s32[]{:S(2)}) async-start(s8[5505024]{0:T(1024)(128)(4,1)} %bitcast.66), calls=%async_computation.22 | async-start | bytes 8388608
  11.2 20.9 %copy-start.33 = (f32[2048]{0:T(1024)}, f32[2048]{0:T(1024)S(1)}, u32[]{:S(2)}) copy-start(f32[2048]{0:T(1024)S(1)} %add_rsqrt_fusion) | copy-start | bytes 24580
  11.2 11.7 %slice-start.5 = ((s8[5505024]{0:T(1024)(128)(4,1)}), s8[1310720]{0:T(1024)(128)(4,1)S(1)}, s32[]{:S(2)}) async-start(s8[5505024]{0:T(1024)(128)(4,1)} %bitcast.66), calls=%async_computation.23 | async-start | bytes 2621440
  11.2 11.6 %copy-start.26 = (bf16[1,2048,768]{2,1,0:T(8,128)(2,1)S(1)}, bf16[1,2048,768]{2,1,0:T(8,128)(2,1)}, u32[]{:S(2)}) copy-start(bf16[1,2048,768]{2,1,0:T(8,128)(2,1)} %param.11) | copy-start | bytes 9437188
  22.8 24.6 %slice-start = ((s8[5505024]{0:T(1024)(128)(4,1)}), s8[4194304]{0:T(1024)(128)(4,1)S(1)}, s32[]{:S(2)}) async-start(s8[5505024]{0:T(1024)(128)(4,1)} %bitcast.62), calls=%async_computation.18 | async-start | bytes 8388608
  32.0 15.4 %slice-start.1 = ((s8[5505024]{0:T(1024)(128)(4,1)}), s8[1310720]{0:T(1024)(128)(4,1)S(1)}, s32[]{:S(2)}) async-start(s8[5505024]{0:T(1024)(128)(4,1)} %bitcast.62), calls=%async_computation.19 | async-start | bytes 2621440
  56.1 1.7 copy-start.28
  56.1 1.7 copy-start.31
  68.9 23.3 %copy-start.27 = (bf16[1,2048,768]{2,1,0:T(8,128)(2,1)S(1)}, bf16[1,2048,768]{2,1,0:T(8,128)(2,1)}, u32[]{:S(2)}) copy-start(bf16[1,2048,768]{2,1,0:T(8,128)(2,1)} %param.12) | copy-start | bytes 9437188
  106.7 16.6 %copy-start.29 = (bf16[2048,768]{0,1:T(8,128)(2,1)S(1)}, bf16[2048,768]{0,1:T(8,128)(2,1)}, u32[]{:S(2)}) copy-start(bf16[2048,768]{0,1:T(8,128)(2,1)} %copy-done.28) | copy-start | bytes 9437188
  106.7 147.3 %reduce-scatter.9.cloned.1.call-start = ((), (), s32[]{:S(2)}) async-start(), calls=%async_computation.7 | async-start | bytes 2924544 | tf_op jit(solution)/shard_map/reduce_scatter | solution.py:131
  123.2 204.3 %reduce-scatter.11.cloned.1.call-start = ((), (), s32[]{:S(2)}) async-start(), calls=%async_computation.8 | async-start | bytes 2924544 | tf_op jit(solution)/shard_map/reduce_scatter | solution.py:131
  133.6 267.9 %reduce-scatter.13.cloned.1.call-start = ((), (), s32[]{:S(2)}) async-start(), calls=%async_computation.9 | async-start | bytes 2924544 | tf_op jit(solution)/shard_map/reduce_scatter | solution.py:131
  133.7 15.2 %slice-start.2 = ((s8[5505024]{0:T(1024)(128)(4,1)}), s8[1310720]{0:T(1024)(128)(4,1)S(1)}, s32[]{:S(2)}) async-start(s8[5505024]{0:T(1024)(128)(4,1)} %bitcast.64), calls=%async_computation.20 | async-start | bytes 2621440
  138.6 10.3 %slice-start.3 = ((s8[5505024]{0:T(1024)(128)(4,1)}), s8[4194304]{0:T(1024)(128)(4,1)S(1)}, s32[]{:S(2)}) async-start(s8[5505024]{0:T(1024)(128)(4,1)} %bitcast.64), calls=%async_computation.21 | async-start | bytes 8388608
  148.9 13.8 %copy-start.32 = (f32[2048]{0:T(1024)S(1)}, f32[2048]{0:T(1024)}, u32[]{:S(2)}) copy-start(f32[2048]{0:T(1024)} %copy-done.31) | copy-start | bytes 24580
  168.7 1.7 copy-start.30
  179.7 12.0 %copy-start.25 = (bf16[1,2048,768]{1,2,0:T(8,128)(2,1)S(1)}, bf16[1,2048,768]{1,2,0:T(8,128)(2,1)}, u32[]{:S(2)}) copy-start(bf16[1,2048,768]{1,2,0:T(8,128)(2,1)} %copy-done.24) | copy-start | bytes 9437188
  179.7 12.0 %copy-start.34 = (f32[2048]{0:T(1024)S(1)}, f32[2048]{0:T(1024)}, u32[]{:S(2)}) copy-start(f32[2048]{0:T(1024)} %copy-done.33) | copy-start | bytes 24580
  179.7 295.7 %reduce-scatter.15.cloned.1.call-start = ((), (), s32[]{:S(2)}) async-start(), calls=%async_computation.10 | async-start | bytes 2924544 | tf_op jit(solution)/shard_map/reduce_scatter | solution.py:131
  188.6 3.1 copy-start.35
  203.2 346.0 %reduce-scatter.17.cloned.1.call-start = ((), (), s32[]{:S(2)}) async-start(), calls=%async_computation.11 | async-start | bytes 2924544 | tf_op jit(solution)/shard_map/reduce_scatter | solution.py:131
  220.1 372.3 %all-gather.17.cloned.1.call-start = ((), (), s32[]{:S(2)}) async-start(), calls=%async_computation.17 | async-start | bytes 2924544 | tf_op jit(solution)/shard_map/all_gather | solution.py:135
  220.9 414.1 %all-gather.13.cloned.1.call-start = ((), (), s32[]{:S(2)}) async-start(), calls=%async_computation.15 | async-start | bytes 2924544 | tf_op jit(solution)/shard_map/all_gather | solution.py:135
  254.0 423.6 %all-gather.9.cloned.1.call-start = ((), (), s32[]{:S(2)}) async-start(), calls=%async_computation.13 | async-start | bytes 2924544 | tf_op jit(solution)/shard_map/all_gather | solution.py:135
  327.6 392.5 %all-gather.15.cloned.1.call-start = ((), (), s32[]{:S(2)}) async-start(), calls=%async_computation.16 | async-start | bytes 2924544 | tf_op jit(solution)/shard_map/all_gather | solution.py:135
  401.5 361.1 %all-gather.11.cloned.1.call-start = ((), (), s32[]{:S(2)}) async-start(), calls=%async_computation.14 | async-start | bytes 2924544 | tf_op jit(solution)/shard_map/all_gather | solution.py:135
  475.4 329.6 %all-gather.7.cloned.1.call-start = ((), (), s32[]{:S(2)}) async-start(), calls=%async_computation.12 | async-start | bytes 2924544 | tf_op jit(solution)/shard_map/all_gather | solution.py:135
  592.4 4.1 copy-start
  596.5 2.6 copy-start.6
  599.1 1.8 copy-start.15
  635.0 4.1 copy-start.2
  639.1 2.6 copy-start.8
  641.7 1.8 copy-start.16
  677.6 4.1 copy-start.4
  681.7 2.6 copy-start.10
  684.3 1.8 copy-start.17
  720.0 4.1 copy-start.1
  724.2 2.6 copy-start.7
  726.7 1.8 copy-start.12
  762.6 4.1 copy-start.3
  766.8 2.6 copy-start.9
  769.3 1.8 copy-start.13
  805.1 4.1 copy-start.5
  809.2 2.6 copy-start.11
  811.8 1.8 copy-start.14
  (6 other events, 5.5 us)
Sparse Core Ops, SparseCore 0:
  106.8 73.0 reduce-scatter.6
  183.6 70.2 reduce-scatter.8
  257.1 70.3 reduce-scatter.10
  331.1 70.3 reduce-scatter.12
  405.0 70.2 reduce-scatter.14
  478.9 70.1 reduce-scatter.16
  551.2 41.1 all-gather.16
  594.4 40.5 all-gather.12
  637.0 40.5 all-gather.8
  679.5 40.5 all-gather.14
  722.0 40.5 all-gather.10
  764.5 40.5 all-gather.6

commit v2 on v0

v2 whole, which is shorter than its diff:
```python
import functools
import math

import jax
import jax.numpy as jnp
from jax import lax
from jax.experimental import pallas as pl
from jax.experimental.pallas import tpu as pltpu
from jax.sharding import PartitionSpec as P

MESH = pl.DeviceIdType.MESH
BLOCK = 256
LANES = 128
SLOTS = 4
BF16, F32 = jnp.bfloat16, jnp.float32
ANY = pl.BlockSpec(memory_space=pl.ANY)
VMEM = pl.BlockSpec(memory_space=pltpu.VMEM)


def dot(a, b, over=((1,), (0,))):
    return lax.dot_general(a, b, (over, ((), ())), preferred_element_type=F32)


def normed(wide):
    return (wide * lax.rsqrt(jnp.mean(wide * wide, -1, keepdims=True) + 1e-6)).astype(BF16)


def forward_kernel(x_ref, dy_ref, wg_ref, wu_ref, wd_ref, a_ref, at_ref, h_ref, dyt_ref, act):
    x = x_ref[0].astype(F32)
    a = normed(x)
    a_ref[0] = a
    at_ref[0] = a.T
    for b in range(wg_ref.shape[2] // BLOCK):
        cols = slice(b * BLOCK, (b + 1) * BLOCK)
        gate, up = dot(a, wg_ref[0, :, cols]), dot(a, wu_ref[0, :, cols])
        act[:, cols] = (gate * jax.nn.sigmoid(gate) * up).astype(BF16)
    dyt_ref[...] = dy_ref[0].T
    h = (x + dot(act[...], wd_ref[0]).astype(BF16).astype(F32)).astype(BF16)
    h_ref[...] = h
    a = normed(h.astype(F32))
    a_ref[1] = a
    at_ref[1] = a.T


def forward(x, dy, wg, wu, wd):
    _, tokens, d = x.shape
    ff = wg.shape[2]
    rows = min(512, tokens)
    tall = pl.BlockSpec((1, rows, d), lambda i: (0, i, 0))
    out = [((2, tokens, d), (2, rows, d), lambda i: (0, i, 0)), ((2, d, tokens), (2, d, rows), lambda i: (0, 0, i))]
    out += [((tokens, d), (rows, d), lambda i: (i, 0)), ((d, tokens), (d, rows), lambda i: (0, i))]
    return pl.pallas_call(
        forward_kernel,
        grid=(tokens // rows,),
        out_shape=[jax.ShapeDtypeStruct(s, BF16) for s, _, _ in out],
        in_specs=[tall, tall]
        + [pl.BlockSpec((1, *w.shape[1:]), lambda i: (0, 0, 0), pipeline_mode=pl.Buffered(1)) for w in (wg, wu, wd)],
        out_specs=[pl.BlockSpec(b, m) for _, b, m in out],
        scratch_shapes=[pltpu.VMEM((rows, ff), BF16)],
        compiler_params=pltpu.CompilerParams(vmem_limit_bytes=60 * 2**20),
        cost_estimate=pl.CostEstimate(flops=6 * tokens * d * ff, bytes_accessed=2 * (9 * tokens * d + 3 * d * ff), transcendentals=tokens * ff),
        name="forward",
    )(x, dy, wg, wu, wd)


def places(side):
    me = lax.axis_index("dp")
    x, y = me // side, me % side
    along_x = lambda d: lax.rem(x + side + d, side) * side + y
    along_y = lambda d: x * side + lax.rem(y + side + d, side)
    return ((x, y, along_x, along_y), (y, x, along_y, along_x))


def backward_kernel(side, a_hbm, at_hbm, h_hbm, dy_hbm, dyt_hbm, wg_hbm, wu_hbm, wd_hbm, out_ref, sq_ref, *scratch):
    (A, AT, H, DY, DYT, ACT, DG, DU, WB, WD, WG1, WU1, TERM, R1, R2, R3, R4, ACC, SA, SB, load_sems, w_sems, send_sems, recv_sems) = scratch
    tokens, d = A.shape
    ff = DG.shape[1]
    nb = ff // BLOCK
    chunks = 2 * nb
    rows = min(512, tokens)
    pr = d // side**2
    spots = places(side)
    wrap = lambda v: lax.rem(v, side)

    def remote(src, dst, stage, slot, h, way, to):
        return pltpu.make_async_remote_copy(
            src_ref=src, dst_ref=dst, send_sem=send_sems.at[stage, slot, h, way], recv_sem=recv_sems.at[stage, slot, h, way],
            device_id={"dp": to}, device_id_type=MESH,
        )

    def message(stage, slot, h, way):
        p, q, to_p, to_q = spots[h]
        step = 1 - 2 * way
        if stage == 0:
            return remote(TERM.at[slot, h, wrap(p + 2), pl.ds(2 * way, 2)], R1.at[slot, h, way], 0, slot, h, way, to_p(step))
        if stage == 1:
            return remote(TERM.at[slot, h, wrap(p + side + step)], R2.at[slot, h, way], 1, slot, h, way, to_p(step))
        if stage == 2:
            part = pl.ds(2 * way, 2 - way)
            return remote(SA.at[slot, h, part], R3.at[slot, h, part], 2, slot, h, way, to_q(step))
        return remote(SB.at[slot, h, way], R4.at[slot, h, way], 3, slot, h, way, to_q(step))

    def both(stage, slot, h, what):
        for way in range(2):
            getattr(message(stage, slot, h, way), what)()

    def stage0(c):
        for h in range(2):
            both(0, c % SLOTS, h, "start")

    def stage1(c):
        slot = c % SLOTS
        for h in range(2):
            p = spots[h][0]
            both(0, slot, h, "wait_recv")
            both(0, slot, h, "wait_send")
            for way, at in ((0, wrap(p + 1)), (1, wrap(p + side - 1))):
                half = pl.ds(2 * way, 2)
                TERM[slot, h, at, half] = (TERM[slot, h, at, half].astype(F32) + R1[slot, h, way].astype(F32)).astype(BF16)
            both(1, slot, h, "start")

    def stage2(c):
        slot = c % SLOTS
        for h in range(2):
            p, q = spots[h][:2]
            both(1, slot, h, "wait_recv")
            both(1, slot, h, "wait_send")
            for o in range(side):
                ACC[slot, h, o] = TERM[slot, h, p, o].astype(F32) + R2[slot, h, 0, o].astype(F32) + R2[slot, h, 1, o].astype(F32)
            SA[slot, h] = ACC[slot, h, wrap(q + 2)].astype(BF16)
            both(2, slot, h, "start")

    def stage3(c):
        slot = c % SLOTS
        for h in range(2):
            q = spots[h][1]
            both(2, slot, h, "wait_recv")
            both(2, slot, h, "wait_send")
            after, before = wrap(q + 1), wrap(q + side - 1)
            SB[slot, h, 0, 0:2] = (ACC[slot, h, after, 0:2] + R3[slot, h, 0:2].astype(F32)).astype(BF16)
            SB[slot, h, 0, 2:3] = ACC[slot, h, after, 2:3].astype(BF16)
            SB[slot, h, 1, 0:2] = ACC[slot, h, before, 0:2].astype(BF16)
            SB[slot, h, 1, 2:3] = (ACC[slot, h, before, 2:3] + R3[slot, h, 2:3].astype(F32)).astype(BF16)
            both(3, slot, h, "start")

    def stage4(c):
        slot = c % SLOTS
        for h in range(2):
            q = spots[h][1]
            both(3, slot, h, "wait_recv")
            both(3, slot, h, "wait_send")
            g = (ACC[slot, h, q] + R4[slot, h, 0].astype(F32) + R4[slot, h, 1].astype(F32)).astype(BF16)
            out_ref[h, c] = g
            g = g.astype(F32)
            sq_ref[...] += g[0] * g[0] + g[1] * g[1] + g[2] * g[2]

    def load(which, l=1):
        src, dst = {"A": (a_hbm.at[l], A), "AT": (at_hbm.at[l], AT), "H": (h_hbm, H), "DY": (dy_hbm.at[0], DY), "DYT": (dyt_hbm, DYT),
                    "WG1": (wg_hbm.at[1], WG1), "WU1": (wu_hbm.at[1], WU1)}[which]
        return pltpu.make_async_copy(src, dst, load_sems.at[("A", "AT", "H", "DY", "DYT", "WG1", "WU1").index(which)])

    def weights(i, what):
        l, at, slot = 1 - i // nb, pl.multiple_of((i % nb) * BLOCK, BLOCK), i % 2
        for j, (src, dst) in enumerate((
            (wg_hbm.at[l, :, pl.ds(at, BLOCK)], WB.at[slot, 0]),
            (wu_hbm.at[l, :, pl.ds(at, BLOCK)], WB.at[slot, 1]),
            (wd_hbm.at[l, pl.ds(at, BLOCK), :], WD.at[slot]),
        )):
            getattr(pltpu.make_async_copy(src, dst, w_sems.at[slot, j]), what)()

    def middle():
        load("A", 0).start()
        load("AT", 0).start()
        for which in ("H", "WG1", "WU1"):
            load(which).wait()
        for t in range(tokens // rows):
            at = slice(t * rows, (t + 1) * rows)
            by_a = dot(DG[at, :], WG1[...], ((1,), (1,))).astype(BF16).astype(F32)
            by_a = (by_a + dot(DU[at, :], WU1[...], ((1,), (1,))).astype(BF16).astype(F32)).astype(BF16).astype(F32)
            wide = H[at, :].astype(F32)
            scale = lax.rsqrt(jnp.mean(wide * wide, -1, keepdims=True) + 1e-6)
            by_scale = jnp.sum(by_a * wide, -1, keepdims=True)
            by_wide = (by_a * scale - wide * (by_scale * scale * scale * scale * (1.0 / d))).astype(BF16).astype(F32)
            by_h = (DY[at, :].astype(F32) + by_wide).astype(BF16)
            DY[at, :] = by_h
            DYT[:, at] = by_h.T
        load("A", 0).wait()
        load("AT", 0).wait()

    def compute(i):
        slot, ws = i % SLOTS, i % 2
        cols = pl.ds(pl.multiple_of((i % nb) * BLOCK, BLOCK), BLOCK)
        weights(i, "wait")

        @pl.when(i + 1 < chunks)
        def _():
            weights(i + 1, "start")

        for t in range(tokens // rows):
            at = slice(t * rows, (t + 1) * rows)
            gate, up = dot(A[at, :], WB[ws, 0]), dot(A[at, :], WB[ws, 1])
            by_act = dot(DY[at, :], WD[ws], ((1,), (1,))).astype(BF16).astype(F32)
            sig = jax.nn.sigmoid(gate)
            silu = gate * sig
            ACT[at, :] = (silu * up).astype(BF16)
            DU[at, cols] = (by_act * silu).astype(BF16)
            DG[at, cols] = (by_act * up * (sig * (1.0 + gate * (1.0 - sig)))).astype(BF16)

        @pl.when(i == 0)
        def _():
            load("AT").wait()
            load("DYT").wait()

        for j, (left, right) in enumerate(((AT, DG[:, cols]), (AT, DU[:, cols]), (DYT, ACT[...]))):
            g = dot(left[...], right).astype(BF16)
            for o in range(side):
                piece = g[o * side * pr : (o + 1) * side * pr].reshape(side, pr, BLOCK)
                for h in range(2):
                    TERM[slot, h, o, :, j] = piece[:, :, h * LANES : (h + 1) * LANES]

    for which in ("A", "DY", "AT", "DYT", "H", "WG1", "WU1"):
        load(which).start()
    weights(0, "start")
    barrier = pltpu.get_barrier_semaphore()
    for h in range(2):
        for step in (1, -1):
            pl.semaphore_signal(barrier, inc=1, device_id={"dp": spots[h][2](step)}, device_id_type=MESH)
    sq_ref[...] = jnp.zeros_like(sq_ref)
    load("A").wait()
    load("DY").wait()
    pl.semaphore_wait(barrier, 4)

    @pl.loop(0, chunks + 4)
    def _(i):
        pl.when(i == nb)(middle)
        pl.when(i < chunks)(lambda: compute(i))
        pl.when(i < chunks)(lambda: stage0(i))
        for lag, stage in enumerate((stage1, stage2, stage3, stage4), 1):
            pl.when((i >= lag) & (i < chunks + lag))(functools.partial(stage, i - lag))


def backward(side, a, at, h, dy, dyt, wg, wu, wd):
    _, tokens, d = a.shape
    ff = wg.shape[2]
    chunks = 2 * (ff // BLOCK)
    pr = d // side**2
    piece = (3, pr, LANES)
    v = pltpu.VMEM
    sems = pltpu.SemaphoreType.DMA
    return pl.pallas_call(
        functools.partial(backward_kernel, side),
        out_shape=[jax.ShapeDtypeStruct((2, chunks, *piece), BF16), jax.ShapeDtypeStruct((pr, LANES), F32)],
        in_specs=[ANY] * 8,
        out_specs=[VMEM] * 2,
        scratch_shapes=[
            v((tokens, d), BF16), v((d, tokens), BF16), v((tokens, d), BF16), v((tokens, d), BF16), v((d, tokens), BF16),
            v((tokens, BLOCK), BF16), v((tokens, ff), BF16), v((tokens, ff), BF16),
            v((2, 2, d, BLOCK), BF16), v((2, BLOCK, d), BF16), v((d, ff), BF16), v((d, ff), BF16),
            v((SLOTS, 2, side, side, *piece), BF16), v((SLOTS, 2, 2, 2, *piece), BF16), v((SLOTS, 2, 2, side, *piece), BF16),
            v((SLOTS, 2, *piece), BF16), v((SLOTS, 2, 2, *piece), BF16), v((SLOTS, 2, side, *piece), F32),
            v((SLOTS, 2, *piece), BF16), v((SLOTS, 2, 2, *piece), BF16),
            sems((7,)), sems((2, 3)), sems((4, SLOTS, 2, 2)), sems((4, SLOTS, 2, 2)),
        ],
        compiler_params=pltpu.CompilerParams(collective_id=0, has_side_effects=True, vmem_limit_bytes=67043328),
        cost_estimate=pl.CostEstimate(flops=28 * tokens * d * ff, bytes_accessed=2 * (7 * tokens * d + 8 * d * ff), transcendentals=2 * tokens * ff),
        name="backward",
    )(a, at, h, dy, dyt, wg, wu, wd)


def gather_kernel(side, count, groups, shard_ref, sq_ref, g_ref, f_ref, mine, slots, sq_sems, send_sems, recv_sems, own_sems):
    n = side * side
    me = lax.axis_index("dp")
    spots = places(side)
    wrap = lambda v: lax.rem(v + side, side)
    barrier = pltpu.get_barrier_semaphore()
    for d in range(1, n):
        pl.semaphore_signal(barrier, inc=1, device_id={"dp": lax.rem(me + d, n)}, device_id_type=MESH)
    squares = jnp.broadcast_to(jnp.sum(sq_ref[...], axis=0, keepdims=True), mine.shape)
    mine[...] = squares
    slots[me] = squares
    own = []
    for h, (p, q, _, _) in enumerate(spots):
        own.append(pltpu.make_async_copy(shard_ref.at[h], g_ref.at[h, p, q], own_sems.at[h]))
        own[-1].start()
    pl.semaphore_wait(barrier, n - 1)
    sent = []
    for d in range(1, n):
        copy = pltpu.make_async_remote_copy(
            src_ref=mine, dst_ref=slots.at[me], send_sem=sq_sems.at[0, d], recv_sem=sq_sems.at[1, d],
            device_id={"dp": lax.rem(me + d, n)}, device_id_type=MESH,
        )
        copy.start()
        sent.append(copy)
    factors = list(sent)

    def piece(k, h, dp, dq):
        p, q = spots[h][:2]
        return g_ref.at[h, wrap(p - dp), wrap(q - dq), pl.ds(*groups[k])]

    def send(k, h, dp, dq, to, own=False, come=None):
        src = shard_ref.at[h, pl.ds(*groups[k])] if own else piece(k, h, dp, dq)
        index = come[0] * side + come[1]
        copy = pltpu.make_async_remote_copy(
            src_ref=src, dst_ref=piece(k, h, dp, dq), send_sem=send_sems.at[k, h, len(sends[k, h])], recv_sem=recv_sems.at[k, h, index],
            device_id={"dp": to}, device_id_type=MESH,
        )
        copy.start()
        sends[k, h].append(copy)

    def arrived(k, h, dp, dq):
        ref = piece(k, h, dp, dq)
        pltpu.make_async_remote_copy(
            src_ref=ref, dst_ref=ref, send_sem=send_sems.at[k, h, 0], recv_sem=recv_sems.at[k, h, dp * side + dq],
            device_id={"dp": me}, device_id_type=MESH,
        ).wait_recv()

    sends = {(k, h): [] for k in range(len(groups)) for h in range(2)}
    last = side - 1

    def across(k, h, dq, own=False):
        to_p = spots[h][2]
        send(k, h, 0, dq, to_p(1), own, (1, dq))
        send(k, h, 0, dq, to_p(-1), own, (last, dq))

    def begin(k):
        for h in range(2):
            to_q = spots[h][3]
            send(k, h, 0, 0, to_q(1), True, (0, 1))
            send(k, h, 0, 0, to_q(-1), True, (0, last))
        for h in range(2):
            across(k, h, 0, True)

    def first(k):
        for h in range(2):
            to_q = spots[h][3]
            arrived(k, h, 0, 1)
            arrived(k, h, 0, last)
            if (k + h) % 2:
                send(k, h, 0, last, to_q(-1), come=(0, 2))
            else:
                send(k, h, 0, 1, to_q(1), come=(0, 2))
            across(k, h, 1)
            across(k, h, last)

    def second(k):
        for h in range(2):
            arrived(k, h, 0, 2)
            across(k, h, 2)

    def third(k):
        for h in range(2):
            to_p = spots[h][2]
            for dq in (0, 1, last, 2):
                arrived(k, h, 1, dq)
                arrived(k, h, last, dq)
                if dq % 2:
                    send(k, h, last, dq, to_p(-1), come=(2, dq))
                else:
                    send(k, h, 1, dq, to_p(1), come=(2, dq))

    def fourth(k):
        for h in range(2):
            for dq in range(side):
                arrived(k, h, 2, dq)

    for s in range(len(groups) + 3):
        for lag, stages in enumerate(((begin,), (first, second), (third,), (fourth,))):
            if 0 <= s - lag < len(groups):
                for stage in stages:
                    stage(s - lag)
        if s == 1:
            for copy in factors:
                copy.wait_recv()
            total = jnp.zeros((8, LANES), F32)
            for i in range(n):
                total = total + slots[i]
            total = jnp.sum(total[0:1], axis=1, keepdims=True)
            f_ref[...] = jnp.broadcast_to(jnp.minimum(1.0, 0.5 * lax.rsqrt(total / count + 1e-30)), f_ref.shape)
    for copies in sends.values():
        sent.extend(copies)
    for copy in sent:
        copy.wait_send()
    for copy in own:
        copy.wait()


def gather(side, count, shard, sq):
    chunks = shard.shape[1]
    size = max(1, chunks // 4 + (chunks % 4 > 0))
    groups = [(c, min(size, chunks - c)) for c in range(0, chunks, size)]
    n = side * side
    sems = pltpu.SemaphoreType.DMA
    return pl.pallas_call(
        functools.partial(gather_kernel, side, count, groups),
        out_shape=[jax.ShapeDtypeStruct((2, side, side, *shard.shape[1:]), BF16), jax.ShapeDtypeStruct((8, LANES), F32)],
        in_specs=[VMEM, VMEM],
        out_specs=[ANY, VMEM],
        scratch_shapes=[
            pltpu.VMEM((8, LANES), F32), pltpu.VMEM((n, 8, LANES), F32), sems((2, n)),
            sems((len(groups), 2, n - 1)), sems((len(groups), 2, n)), sems((2,)),
        ],
        compiler_params=pltpu.CompilerParams(collective_id=1, has_side_effects=True, vmem_limit_bytes=60 * 2**20),
        cost_estimate=pl.CostEstimate(flops=10**8, bytes_accessed=2 * n * shard.size, transcendentals=0),
        name="gather",
    )(shard, sq)


def adamw(f, g, w, m, v):
    g = g.astype(F32) * f
    m = 0.9 * m + 0.1 * g
    v = 0.95 * v + 0.05 * g * g
    w = w.astype(F32)
    return (w - 0.02 * (m * lax.rsqrt(v + 1e-8) + 0.1 * w)).astype(BF16), m, v


def wide_kernel(f_ref, g_ref, *refs):
    f = f_ref[0:1, 0:1]
    for j in range(2):
        w, m, v, nw, nm, nv = refs[j::2]
        _, _, places_, nb, _, pr, _ = g_ref.shape
        for b in range(nb):
            for h in range(2):
                cols = slice((2 * b + h) * LANES, (2 * b + h + 1) * LANES)
                g = g_ref[h, 0, :, b, j].reshape(places_ * pr, LANES)
                nw[0, :, cols], nm[0, :, cols], nv[0, :, cols] = adamw(f, g, w[0, :, cols], m[0, :, cols], v[0, :, cols])


def tall_kernel(f_ref, g_ref, w, m, v, nw, nm, nv):
    f = f_ref[0:1, 0:1]
    _, side, _, _, _, pr, _ = g_ref.shape
    for h in range(2):
        rows = slice(h * LANES, (h + 1) * LANES)
        g = g_ref[h, :, :, 0, 0].reshape(side * side * pr, LANES).T
        nw[0, rows, :], nm[0, rows, :], nv[0, rows, :] = adamw(f, g, w[0, rows, :], m[0, rows, :], v[0, rows, :])


def update_wide(f, g, weights, m, v):
    arrays = (*weights, *m, *v)
    layers, d, ff = weights[0].shape
    _, side, _, chunks, _, pr, _ = g.shape
    nb = chunks // layers
    block = pl.BlockSpec((1, d // side, ff), lambda l, i: (l, i, 0))
    return pl.pallas_call(
        wide_kernel,
        grid=(layers, side),
        out_shape=[jax.ShapeDtypeStruct(a.shape, a.dtype) for a in arrays],
        in_specs=[pl.BlockSpec((8, LANES), lambda l, i: (0, 0)),
                  pl.BlockSpec((2, 1, side, nb, 2, pr, LANES), lambda l, i: (0, i, 0, layers - 1 - l, 0, 0, 0))] + [block] * 6,
        out_specs=[block] * 6,
        compiler_params=pltpu.CompilerParams(vmem_limit_bytes=60 * 2**20),
        cost_estimate=pl.CostEstimate(flops=30 * layers * d * ff, bytes_accessed=44 * layers * d * ff, transcendentals=2 * layers * d * ff),
        name="update_wide",
    )(f, g, *arrays)


def update_tall(f, g, w, m, v):
    layers, ff, d = w.shape
    _, side, _, chunks, _, pr, _ = g.shape
    nb = chunks // layers
    block = pl.BlockSpec((1, BLOCK, d), lambda l, b: (l, b, 0))
    return pl.pallas_call(
        tall_kernel,
        grid=(layers, nb),
        out_shape=[jax.ShapeDtypeStruct(a.shape, a.dtype) for a in (w, m, v)],
        in_specs=[pl.BlockSpec((8, LANES), lambda l, b: (0, 0)),
                  pl.BlockSpec((2, side, side, 1, 1, pr, LANES), lambda l, b: (0, 0, 0, (layers - 1 - l) * nb + b, 2, 0, 0))] + [block] * 3,
        out_specs=[block] * 3,
        compiler_params=pltpu.CompilerParams(vmem_limit_bytes=60 * 2**20),
        cost_estimate=pl.CostEstimate(flops=15 * layers * d * ff, bytes_accessed=22 * layers * d * ff, transcendentals=layers * d * ff),
        name="update_tall",
    )(f, g, w, m, v)


def solution(mesh):
    side = math.isqrt(mesh.shape["dp"])

    def step(x, dy, wg, wu, wd, mg, mu, md, vg, vu, vd):
        a, at, h, dyt = forward(x, dy, wg, wu, wd)
        shard, sq = backward(side, a, at, h, dy, dyt, wg, wu, wd)
        g, f = gather(side, float(wg.size + wu.size + wd.size), shard, sq)
        new = update_wide(f, g, (wg, wu), (mg, mu), (vg, vu))
        nwd, nmd, nvd = update_tall(f, g, wd, md, vd)
        return new[0], new[1], nwd, new[2], new[3], nmd, new[4], new[5], nvd

    return jax.shard_map(
        step,
        mesh=mesh,
        in_specs=(P(("rep", "dp"), None, None),) * 2 + (P(None, None, None),) * 9,
        out_specs=(P("rep", None, None),) * 9,
        check_vma=False,
    )
```

time: 512 us -> 317 us (0.62)
  the two profiles are of different devices: /device:TPU:97 before, /device:TPU:96 now
where the time goes in v2:
time: 317 us
  Pallas kernels  316 us (100%)
    pallas_call x1, Pallas kernels, backward(): pl.pallas_call(functools.partial(backward_kernel, side), out_shape=[jax.S...  131 us
    pallas_call x1, Pallas kernels, gather(): pl.pallas_call(functools.partial(gather_kernel, side, count, groups), out...  93.5 us
    pallas_call x1, Pallas kernels, update_wide(): pl.pallas_call(wide_kernel, grid=(layers, side), out_shape=[jax.ShapeDtyp...  39.2 us
    pallas_call x1, Pallas kernels, forward(): pl.pallas_call(forward_kernel, grid=(tokens // rows,), out_shape=[jax.Sha...  26.8 us
    pallas_call x1, Pallas kernels, update_tall(): pl.pallas_call(tall_kernel, grid=(layers, nb), out_shape=[jax.ShapeDtypeS...  25.7 us

profile of v2, /device:TPU:96, one launch (start us, length us, event | category | flops | bytes accessed | tf_op | source)
XLA Modules:
  0.0 317.1 jit_solution(14056800151059769529)
XLA Ops:
  0.6 26.8 %forward.1 = (bf16[2,2048,768]{2,1,0:T(8,128)(2,1)}, bf16[2,768,2048]{2,1,0:T(8,128)(2,1)}, bf16[2048,768]{1,0:T(8,128)(2,1)}, bf16[768,2048]{1,0:T(8,128)(2,1)}) custom-call(bf16[1,2048,768]{2,1,0:T(8,128)(2,1)} %x_ref.1, bf16[1,2048,768]{2,1,0:T(8,128)(2,1)} %dy_hbm.1, bf16[2,768,1792]{2,1,0:T(8,128)(2,1)} %refs_0_.1, bf16[2,768,1792]{2,1,0:T(8,128)(2,1)} %refs_1_.1, ...), custom_call_target="tpu_custom_call" | custom-call | flops 16911433728 | bytes 36569088 | tf_op jit(solution)/shard_map/forward/pallas_call | solution.py:52
  27.4 131.1 %backward.1 = (bf16[2,14,3,48,128]{4,3,2,1,0:T(8,128)(2,1)}, f32[48,128]{1,0:T(8,128)}) custom-call(bf16[2,2048,768]{2,1,0:T(8,128)(2,1)} %get-tuple-element.26.a_hbm, bf16[2,768,2048]{2,1,0:T(8,128)(2,1)} %get-tuple-element.27.at_hbm, bf16[2048,768]{1,0:T(8,128)(2,1)} %get-tuple-element.28.h_hbm, bf16[1,2048,768]{2,1,0:T(8,128)(2,1)} %dy_hbm.1, ...), custom_call_target="tpu_custom_call" | custom-call | flops 78920024064 | bytes 44040192 | tf_op jit(solution)/shard_map/backward/pallas_call | solution.py:250
  158.6 93.5 %gather.1 = (bf16[2,4,4,14,3,48,128]{6,5,4,3,2,1,0:T(8,128)(2,1)}, f32[8,128]{1,0:T(8,128)}) custom-call(bf16[2,14,3,48,128]{4,3,2,1,0:T(8,128)(2,1)} %get-tuple-element.30.shard_ref, f32[48,128]{1,0:T(8,128)} %get-tuple-element.31.sq_ref), custom_call_target="tpu_custom_call" | custom-call | flops 100000000 | bytes 16515072 | tf_op jit(solution)/shard_map/gather/pallas_call | solution.py:393
  252.0 25.7 %update_tall.1 = (bf16[2,1792,768]{2,1,0:T(8,128)(2,1)}, f32[2,1792,768]{2,1,0:T(8,128)}, f32[2,1792,768]{2,1,0:T(8,128)}) custom-call(f32[8,128]{1,0:T(8,128)} %get-tuple-element.32.f_ref, bf16[2,4,4,14,3,48,128]{6,5,4,3,2,1,0:T(8,128)(2,1)} %get-tuple-element.33.g_ref, bf16[2,1792,768]{2,1,0:T(8,128)(2,1)} %w.1, f32[2,1792,768]{2,1,0:T(8,128)} %m.1, ...), custom_call_target="tpu_custom_call" | custom-call | flops 41287680 | bytes 60555264 | tf_op jit(solution)/shard_map/update_tall/pallas_call | solution.py:461
  277.7 39.2 %update_wide.1 = (bf16[2,768,1792]{2,1,0:T(8,128)(2,1)}, bf16[2,768,1792]{2,1,0:T(8,128)(2,1)}, f32[2,768,1792]{2,1,0:T(8,128)}, f32[2,768,1792]{2,1,0:T(8,128)}...) custom-call(f32[8,128]{1,0:T(8,128)} %get-tuple-element.32.f_ref, ...), custom_call_target="tpu_custom_call" | custom-call | flops 82575360 | bytes 121110528 | tf_op jit(solution)/shard_map/update_wide/pallas_call | solution.py:443
